TPU v7x, 32 devices: a whole 2x2x4 slice. The times are simulated.
32 devices in a mesh: section: 2 (over x), expert: 4 (over y, core), dp: 4 (over z).
Axes of the slice: x: 2, y: 2, z: 4, core: 2. Of those that a mesh axis runs over, the one named last changes fastest.
Arguments:
- x_in: bfloat16 [8, 256, 2048], P(None, ('expert', 'dp'), 'section'), may hold values from -6 to 6
- cotangent: bfloat16 [8, 256, 2048], P(None, ('expert', 'dp'), 'section'), may hold values from -6 to 6
- route_ids: int32 [2, 8, 256, 2], P('section', None, ('expert', 'dp')), may hold values from 0 to 15, all different within a row; in each aligned block of 16 rows (0 to 15, 16 to 31, ..., all dimensions but the last counted through in order) at most 2 rows name the same one
- norm_gain: float32 [2, 2048], P('section'), may hold values from 0.5 to 1.5
- router: bfloat16 [2, 2048, 16], P('section'), may hold values from -0.125 to 0.125
- w_gate_up: bfloat16 [2, 16, 2048, 1024], P('section', ('expert', 'dp')), may hold values from -0.125 to 0.125
- w_down: bfloat16 [2, 16, 512, 2048], P('section', ('expert', 'dp')), may hold values from -0.25 to 0.25
Outputs:
- grad_in: bfloat16 [8, 256, 2048], P(None, ('expert', 'dp'), 'section')
- grad_gate_up: float32 [2, 16, 2048, 1024], P('section', ('expert', 'dp'))
- grad_down: float32 [2, 16, 512, 2048], P('section', ('expert', 'dp'))
- grad_router: float32 [2, 2048, 16], P('section')
- grad_gain: float32 [2, 2048], P('section')
Inputs may be any that keep to these rules, and one draw needn't show every extreme that they name: `route_ids`: each row names two different experts; the 16 rows of one device in one layer and micro-batch name any expert at most 2 times, a bound that some block reaches in some of them.
All inputs are finite; a program needn't handle non-finite values.
Results may differ from a plain program's by a relative error of at most 0.035.
Values may be sent and summed in bfloat16 or wider, within the bound.
A program may use at most 64 MiB of HBM per device.

v0:
```python
import jax
import jax.numpy as jnp
from jax import lax
from jax.sharding import PartitionSpec as P

EPS = 1e-05


def shifted(value, axis, steps):
    count = lax.axis_size(axis)
    leading, last = (max(0, -steps), min(count, count - steps))
    return lax.ppermute(value, axis, [(source, source + steps) for source in range(leading, last)])


def keep_row(stash, position, value, active):
    old_row = lax.dynamic_index_in_dim(stash, position, 0, keepdims=False)
    return lax.dynamic_update_index_in_dim(stash, jnp.where(active, value, old_row), position, 0)


def slot_tables(route_rows, n_expert, capacity):
    experts = jnp.arange(n_expert, dtype=jnp.int32)
    expert_hits = (route_rows[:, :, None] == experts).astype(jnp.int32)
    per_expert = jnp.sum(expert_hits, axis=1)
    before = jnp.cumsum(per_expert, axis=0) - per_expert
    slot_ids = jnp.sum(expert_hits * before[:, None, :], axis=2)
    dest_cell = jnp.transpose(route_rows * capacity + slot_ids)
    cell_ids = jnp.arange(n_expert * capacity, dtype=jnp.int32)
    slot_place = (dest_cell[:, :, None] == cell_ids).astype(jnp.bfloat16)
    return (expert_hits.astype(jnp.float32), slot_place)


def norm_rows(layer_in, gain_vec):
    h_wide = layer_in.astype(jnp.float32)
    inv_rms = lax.rsqrt(jnp.mean(h_wide * h_wide, axis=-1, keepdims=True) + EPS)
    normed = (h_wide * inv_rms * gain_vec).astype(jnp.bfloat16)
    return (h_wide, inv_rms, normed)


def pair_gates(normed, router_mat, expert_hits):
    logits = jnp.dot(normed, router_mat, preferred_element_type=jnp.float32)
    chosen = jnp.sum(expert_hits * logits[:, None, :], axis=2)
    return (
        jax.nn.sigmoid(chosen[:, 0] - chosen[:, 1]),
        jax.nn.sigmoid(chosen[:, 1] - chosen[:, 0]),
    )


def expert_inner(exp_rows, w_gu):
    gate_up = jnp.einsum("sekd,edf->sekf", exp_rows, w_gu, preferred_element_type=jnp.float32)
    half_cols = w_gu.shape[2] // 2
    gate_part = gate_up[..., :half_cols]
    up_part = gate_up[..., half_cols:]
    sigmoid_gate = jax.nn.sigmoid(gate_part)
    hidden = (gate_part * sigmoid_gate * up_part).astype(jnp.bfloat16)
    return (gate_part, up_part, sigmoid_gate, hidden)


def expert_grads(gate_part, up_part, sigmoid_gate, dy_rows, w_gu, w_dn):
    d_hidden = jnp.einsum("sekd,efd->sekf", dy_rows, w_dn, preferred_element_type=jnp.float32)
    silu_gate = gate_part * sigmoid_gate
    silu_slope = sigmoid_gate * (1.0 + gate_part * (1.0 - sigmoid_gate))
    gate_up_grad = jnp.concatenate(
        [d_hidden * up_part * silu_slope, d_hidden * silu_gate], axis=-1
    ).astype(jnp.bfloat16)
    rows_grad = jnp.einsum(
        "sekf,edf->sekd", gate_up_grad, w_gu, preferred_element_type=jnp.float32
    ).astype(jnp.bfloat16)
    return (gate_up_grad, rows_grad)


def local(x_in, cotangent, route_ids, norm_gain, router, w_gate_up, w_down):
    micro_count, tok_rows, _ = x_in.shape
    n_segment = lax.axis_size("section")
    n_rank = lax.axis_size("expert") * lax.axis_size("dp")
    per_rank = w_down.shape[1]
    hidden_width = w_down.shape[2]
    model_width = w_down.shape[3]
    n_expert = per_rank * n_rank
    capacity = tok_rows * 2 * 9 // (8 * n_expert)
    cells = n_expert * capacity
    segment_idx = lax.axis_index("section")
    rows_shape = (n_rank, per_rank, capacity, model_width)
    x_all, top_all = (
        lax.all_gather(x_in, "section", axis=2, tiled=True),
        lax.all_gather(cotangent, "section", axis=2, tiled=True),
    )
    route_all = route_ids[0]
    gain_vec = norm_gain[0]
    router_mat = router[0]
    router_wide = router_mat.astype(jnp.float32)
    w_gu = w_gate_up[0]
    w_dn = w_down[0]
    ticks = micro_count + n_segment - 1

    def expert_forward(piece_rows):
        _, _, _, hidden = expert_inner(piece_rows, w_gu)
        out_rows = jnp.einsum(
            "sekf,efd->sekd", hidden, w_dn, preferred_element_type=jnp.float32
        ).astype(jnp.bfloat16)
        return (
            lax.all_to_all(out_rows, ("expert", "dp"), split_axis=0, concat_axis=0, tiled=True),
            piece_rows,
        )

    def forward_tick(tick_no, state_in):
        received, stash_h, stash_y, stash_x = state_in
        tick_slot = tick_no - segment_idx
        active = (tick_slot >= 0) & (tick_slot < micro_count)
        micro_idx = jnp.clip(tick_slot, 0, micro_count - 1)
        fresh_in = lax.dynamic_index_in_dim(x_all, micro_idx, 0, keepdims=False)
        layer_in = jnp.where(segment_idx == 0, fresh_in, received)
        h_wide, inv_rms, normed = norm_rows(layer_in, gain_vec)
        route_rows = lax.dynamic_index_in_dim(route_all, micro_idx, 0, keepdims=False)
        expert_hits, slot_place = slot_tables(route_rows, n_expert, capacity)
        send_rows = jnp.einsum("ktc,td->cd", slot_place, normed, preferred_element_type=jnp.float32)
        send_rows = send_rows.astype(jnp.bfloat16).reshape(rows_shape)
        returned, landed = expert_forward(
            lax.all_to_all(send_rows, ("expert", "dp"), split_axis=0, concat_axis=0, tiled=True)
        )
        back_flat = returned.reshape(cells, model_width)
        picked = jnp.einsum(
            "ktc,cd->ktd", slot_place, back_flat, preferred_element_type=jnp.float32
        )
        first_gate, second_gate = pair_gates(normed, router_mat, expert_hits)
        layer_out = (
            h_wide + first_gate[:, None] * picked[0] + second_gate[:, None] * picked[1]
        ).astype(jnp.bfloat16)
        passed = shifted(layer_out, "section", 1)
        stash_h = keep_row(stash_h, micro_idx, layer_in, active)
        stash_y = keep_row(stash_y, micro_idx, back_flat, active)
        stash_x = keep_row(stash_x, micro_idx, landed, active)
        return (passed, stash_h, stash_y, stash_x)

    start_fwd = (
        jnp.zeros((tok_rows, model_width), jnp.bfloat16),
        jnp.zeros((micro_count, tok_rows, model_width), jnp.bfloat16),
        jnp.zeros((micro_count, cells, model_width), jnp.bfloat16),
        jnp.zeros((micro_count,) + rows_shape, jnp.bfloat16),
    )
    _, stash_h, stash_y, stash_x = lax.fori_loop(0, ticks, forward_tick, start_fwd)

    def backward_tick(tick_no, state_in):
        received, keep_rows, keep_dy, keep_hidden, keep_dab, stash_grad, acc_router, acc_gain = (
            state_in
        )
        tick_slot = tick_no - (n_segment - 1 - segment_idx)
        active = (tick_slot >= 0) & (tick_slot < micro_count)
        micro_idx = jnp.clip(tick_slot, 0, micro_count - 1)
        fresh_top = lax.dynamic_index_in_dim(top_all, micro_idx, 0, keepdims=False)
        grad_top = jnp.where(segment_idx == n_segment - 1, fresh_top, received)
        grad_wide = grad_top.astype(jnp.float32)
        layer_in = lax.dynamic_index_in_dim(stash_h, micro_idx, 0, keepdims=False)
        h_wide, inv_rms, normed = norm_rows(layer_in, gain_vec)
        route_rows = lax.dynamic_index_in_dim(route_all, micro_idx, 0, keepdims=False)
        expert_hits, slot_place = slot_tables(route_rows, n_expert, capacity)
        first_gate, second_gate = pair_gates(normed, router_mat, expert_hits)
        gates = jnp.stack([first_gate, second_gate])
        scaled = (gates[:, :, None] * grad_wide[None]).astype(jnp.bfloat16)
        dy_send = jnp.einsum("ktc,ktd->cd", slot_place, scaled, preferred_element_type=jnp.float32)
        dy_send = dy_send.astype(jnp.bfloat16).reshape(rows_shape)
        exp_rows = lax.dynamic_index_in_dim(stash_x, micro_idx, 0, keepdims=False)
        dy_rows = lax.all_to_all(dy_send, ("expert", "dp"), split_axis=0, concat_axis=0, tiled=True)
        gate_part, up_part, sigmoid_gate, hidden = expert_inner(exp_rows, w_gu)
        gate_up_grad, rows_grad = expert_grads(
            gate_part, up_part, sigmoid_gate, dy_rows, w_gu, w_dn
        )
        back_grad = lax.all_to_all(
            rows_grad, ("expert", "dp"), split_axis=0, concat_axis=0, tiled=True
        )
        back_y = lax.dynamic_index_in_dim(stash_y, micro_idx, 0, keepdims=False)
        keep_dy = keep_row(keep_dy, micro_idx, dy_rows, active)
        keep_hidden = keep_row(keep_hidden, micro_idx, hidden, active)
        keep_dab = keep_row(keep_dab, micro_idx, gate_up_grad, active)
        normed_grad = jnp.einsum(
            "ktc,cd->td",
            slot_place,
            back_grad.reshape(cells, model_width),
            preferred_element_type=jnp.float32,
        )
        picked = jnp.einsum("ktc,cd->ktd", slot_place, back_y, preferred_element_type=jnp.float32)
        gate_grad = jnp.sum(grad_wide[None] * picked, axis=-1)
        logit_grad = first_gate * second_gate * (gate_grad[0] - gate_grad[1])
        logit_cols = logit_grad[:, None] * (expert_hits[:, 0, :] - expert_hits[:, 1, :])
        normed_grad = normed_grad + jnp.dot(
            logit_cols, router_wide.T, precision=lax.Precision.HIGHEST
        )
        router_term = jnp.dot(
            normed.astype(jnp.float32).T, logit_cols, precision=lax.Precision.HIGHEST
        )
        acc_router = acc_router + jnp.where(active, router_term, 0.0)
        acc_gain = acc_gain + jnp.where(
            active, jnp.sum(normed_grad * h_wide * inv_rms, axis=0), 0.0
        )
        scaled_grad = normed_grad * gain_vec
        projection = jnp.mean(scaled_grad * h_wide, axis=-1, keepdims=True)
        input_grad = (
            grad_wide + inv_rms * scaled_grad - h_wide * inv_rms * inv_rms * inv_rms * projection
        )
        grad_sent = input_grad.astype(jnp.bfloat16)
        stash_grad = keep_row(stash_grad, micro_idx, grad_sent, active)
        passed = shifted(grad_sent, "section", -1)
        return (passed, keep_rows, keep_dy, keep_hidden, keep_dab, stash_grad, acc_router, acc_gain)

    start_bwd = (
        jnp.zeros((tok_rows, model_width), jnp.bfloat16),
        stash_x,
        jnp.zeros((micro_count,) + rows_shape, jnp.bfloat16),
        jnp.zeros((micro_count, n_rank, per_rank, capacity, hidden_width), jnp.bfloat16),
        jnp.zeros((micro_count, n_rank, per_rank, capacity, 2 * hidden_width), jnp.bfloat16),
        jnp.zeros((micro_count, tok_rows, model_width), jnp.bfloat16),
        jnp.zeros((model_width, n_expert), jnp.float32),
        jnp.zeros((model_width,), jnp.float32),
    )
    final = lax.fori_loop(0, ticks, backward_tick, start_bwd)
    _, keep_rows, keep_dy, keep_hidden, keep_dab, stash_grad, acc_router, acc_gain = final
    grad_gu = jnp.einsum(
        "msekd,msekf->edf", keep_rows, keep_dab, preferred_element_type=jnp.float32
    )
    grad_dn = jnp.einsum(
        "msekf,msekd->efd", keep_hidden, keep_dy, preferred_element_type=jnp.float32
    )
    sum_router, sum_gain = (
        lax.psum(acc_router.astype(jnp.bfloat16), ("expert", "dp")).astype(jnp.float32),
        lax.psum(acc_gain.astype(jnp.bfloat16), ("expert", "dp")).astype(jnp.float32),
    )
    first_term = jnp.where(segment_idx == 0, stash_grad.astype(jnp.float32), 0.0)
    grad_in = lax.psum_scatter(
        first_term.astype(jnp.bfloat16), "section", scatter_dimension=2, tiled=True
    )
    return (grad_in, grad_gu[None], grad_dn[None], sum_router[None], sum_gain[None])


def solution(mesh):
    in_specs = (
        P(None, ("expert", "dp"), "section"),
        P(None, ("expert", "dp"), "section"),
        P("section", None, ("expert", "dp"), None),
        P("section", None),
        P("section", None, None),
        P("section", ("expert", "dp"), None, None),
        P("section", ("expert", "dp"), None, None),
    )
    out_specs = (
        P(None, ("expert", "dp"), "section"),
        P("section", ("expert", "dp"), None, None),
        P("section", ("expert", "dp"), None, None),
        P("section", None, None),
        P("section", None),
    )
    return jax.shard_map(local, mesh=mesh, in_specs=in_specs, out_specs=out_specs, check_vma=False)
```

profile of v0, /device:TPU:0, one launch (start us, length us, event | category | flops | bytes accessed | tf_op | source)
XLA Modules:
  0.0 863.5 jit_solution(11679668147466827216)
XLA Ops:
  8.1 12.0 %all_gather.6 = bf16[8,16,2048]{2,1,0:T(8,128)(2,1)} all-gather(bf16[8,16,1024]{2,1,0:T(8,128)(2,1)} %param.12), channel_id=1, replica_groups=mesh['section'=2,'expert'=4,'dp'=4] {'section'}, dimensions={2}, use_global_device_ids=true | all-gather | bytes 786432 | tf_op jit(solution)/shard_map/all_gather | solution.py:85
  20.1 8.4 all_gather.7
  32.9 328.9 %while.48 = (s32[]{:T(128)}, bf16[16,2048]{1,0:T(8,128)(2,1)S(1)}, bf16[8,16,2048]{2,1,0:T(8,128)(2,1)S(1)}, bf16[8,32,2048]{2,1,0:T(8,128)(2,1)}, bf16[8,16,1,2...) while((s32[]{:T(128)}, bf16[16,2048]{1,0:T(8,128)(2,1)S(1)}, ...), condition=%wide.region_7.8_spmd, body=%wide.region_0.7_spmd.sunk | while | flops 209598352 | bytes 11630114 | solution.py:140
  36.7 6.4 all-to-all-start
  45.4 5.1 all-to-all-done
  59.1 6.6 all-to-all-done.1
  80.8 5.1 all-to-all-done
  94.5 6.6 all-to-all-done.1
  101.4 4.3 collective-permute-start
  117.1 5.1 all-to-all-done
  130.8 6.5 all-to-all-done.1
  137.8 4.3 collective-permute-start
  153.5 5.1 all-to-all-done
  167.1 6.6 all-to-all-done.1
  174.1 4.3 collective-permute-start
  189.8 5.1 all-to-all-done
  203.5 6.6 all-to-all-done.1
  210.4 4.3 collective-permute-start
  226.1 5.1 all-to-all-done
  239.8 6.6 all-to-all-done.1
  246.7 4.3 collective-permute-start
  262.4 5.1 all-to-all-done
  276.1 6.6 all-to-all-done.1
  283.0 4.3 collective-permute-start
  298.7 5.1 all-to-all-done
  312.4 6.5 all-to-all-done.1
  319.4 4.3 collective-permute-start
  335.1 5.1 all-to-all-done
  348.8 6.5 all-to-all-done.1
  355.7 4.3 collective-permute-start
  366.0 403.9 %while.49 = (s32[]{:T(128)}, bf16[16,2048]{1,0:T(8,128)(2,1)S(1)}, bf16[8,16,1,2,2048]{4,3,1,2,0:T(2,128)(2,1)}, bf16[8,16,1,2,512]{4,1,3,2,0:T(8,128)(2,1)}, bf...) while((s32[]{:T(128)}, bf16[16,2048]{1,0:T(8,128)(2,1)S(1)}, ...), condition=%wide.region_18.19_spmd.clone, body=%wide.region_8.18_spmd.clone.sunk | while | flops 361911744 | bytes 17806364 | solution.py:214
  388.6 5.9 all-to-all-start.3
  396.8 5.1 all-to-all-done.3
  406.6 4.2 collective-permute-done.1
  429.1 3.5 fusion.205
  433.5 5.9 all-to-all-start.3
  441.7 5.1 all-to-all-done.3
  452.2 3.6 collective-permute-done.1
  478.4 5.9 all-to-all-start.3
  486.6 5.1 all-to-all-done.3
  497.1 3.6 collective-permute-done.1
  518.9 3.5 fusion.205
  523.2 5.9 all-to-all-start.3
  531.5 5.1 all-to-all-done.3
  541.9 3.6 collective-permute-done.1
  568.1 5.9 all-to-all-start.3
  576.3 5.1 all-to-all-done.3
  586.8 3.6 collective-permute-done.1
  613.0 5.9 all-to-all-start.3
  621.2 5.1 all-to-all-done.3
  631.7 3.6 collective-permute-done.1
  653.5 3.5 fusion.205
  657.9 5.9 all-to-all-start.3
  666.1 5.1 all-to-all-done.3
  676.6 3.6 collective-permute-done.1
  702.7 5.9 all-to-all-start.3
  711.0 5.1 all-to-all-done.3
  721.4 3.6 collective-permute-done.1
  747.6 5.9 all-to-all-start.3
  755.9 5.1 all-to-all-done.3
  766.3 3.6 collective-permute-done.1
  772.6 6.2 convolution_bitcast_fusion.1
  778.9 30.9 %psum.15 = bf16[1,2048]{1,0:T(2,128)(2,1)S(1)} all-reduce(bf16[1,2048]{1,0:T(2,128)(2,1)S(1)} %broadcast_in_dim.182), channel_id=1, replica_groups=mesh['section'=2,'expert'=4,'dp'=4] {'expert','dp'}, use_global_device_ids=true, to_apply=%region_21.22 | all-reduce | flops 2048 | bytes 8192 | tf_op jit(solution)/shard_map/psum | solution.py:224
  813.5 41.1 %all-reduce.2.cloned.1.call-done = bf16[1,2048,16]{1,2,0:T(8,128)(2,1)} async-done(((bf16[1,2048,16]{1,2,0:T(8,128)(2,1)}), bf16[1,2048,16]{1,2,0:T(8,128)(2,1)}) %all-reduce.2.cloned.1.call-update) | async-done | bytes 65552 | tf_op jit(solution)/shard_map/psum | solution.py:223
  (697 shorter events, 459.0 us)
Async XLA Ops:
  8.0 24.9 %copy-start.2 = (f32[1,2048]{1,0:T(1,128)S(1)}, f32[1,2048]{1,0:T(1,128)}, u32[]{:S(2)}) copy-start(f32[1,2048]{1,0:T(1,128)} %param.14) | copy-start | bytes 24580
  8.0 24.9 %copy-start = (bf16[1,1,512,2048]{3,2,1,0:T(8,128)(2,1)S(1)}, bf16[1,1,512,2048]{3,2,1,0:T(8,128)(2,1)}, u32[]{:S(2)}) copy-start(bf16[1,1,512,2048]{3,2,1,0:T(8,128)(2,1)} %param.17) | copy-start | bytes 6291460
  8.0 846.5 %all-reduce.2.cloned.1.call-start = ((), (), s32[]{:S(2)}) async-start(), calls=%async_computation.6 | async-start | bytes 131072 | tf_op jit(solution)/shard_map/psum | solution.py:223
  36.7 13.8 %all-to-all-start = ((bf16[16,1,2,2048]{3,2,1,0:T(2,128)(2,1)}), bf16[16,1,2,2048]{3,2,1,0:T(2,128)(2,1)S(1)}, u32[]{:S(2)}, u32[]{:S(2)}) async-start(bf16[16,1,2,2048]{3,2,1,0:T(2,128)(2,1)} %bitcast.324), calls=%async_computation | async-start | bytes 262144 | tf_op jit(solution)/shard_map/while/body/eval_jaxpr/all_to_all | solution.py:118
  54.8 10.9 %all-to-all-start.1 = ((bf16[16,1,2,2048]{3,2,1,0:T(2,128)(2,1)}), bf16[16,1,2,2048]{3,2,1,0:T(2,128)(2,1)S(1)}, u32[]{:S(2)}, u32[]{:S(2)}) async-start(bf16[16,1,2,2048]{3,2,1,0:T(2,128)(2,1)} %copy.84), calls=%async_computation.1 | async-start | bytes 262144 | tf_op jit(solution)/shard_map/while/body/eval_jaxpr/all_to_all | solution.py:101
  66.0 5.3 collective-permute-start
  75.1 10.9 %all-to-all-start = ((bf16[16,1,2,2048]{3,2,1,0:T(2,128)(2,1)}), bf16[16,1,2,2048]{3,2,1,0:T(2,128)(2,1)S(1)}, u32[]{:S(2)}, u32[]{:S(2)}) async-start(bf16[16,1,2,2048]{3,2,1,0:T(2,128)(2,1)} %bitcast.324), calls=%async_computation | async-start | bytes 262144 | tf_op jit(solution)/shard_map/while/body/eval_jaxpr/all_to_all | solution.py:118
  90.2 10.9 %all-to-all-start.1 = ((bf16[16,1,2,2048]{3,2,1,0:T(2,128)(2,1)}), bf16[16,1,2,2048]{3,2,1,0:T(2,128)(2,1)S(1)}, u32[]{:S(2)}, u32[]{:S(2)}) async-start(bf16[16,1,2,2048]{3,2,1,0:T(2,128)(2,1)} %copy.84), calls=%async_computation.1 | async-start | bytes 262144 | tf_op jit(solution)/shard_map/while/body/eval_jaxpr/all_to_all | solution.py:101
  101.4 6.2 collective-permute-start
  111.4 10.9 %all-to-all-start = ((bf16[16,1,2,2048]{3,2,1,0:T(2,128)(2,1)}), bf16[16,1,2,2048]{3,2,1,0:T(2,128)(2,1)S(1)}, u32[]{:S(2)}, u32[]{:S(2)}) async-start(bf16[16,1,2,2048]{3,2,1,0:T(2,128)(2,1)} %bitcast.324), calls=%async_computation | async-start | bytes 262144 | tf_op jit(solution)/shard_map/while/body/eval_jaxpr/all_to_all | solution.py:118
  126.5 10.9 %all-to-all-start.1 = ((bf16[16,1,2,2048]{3,2,1,0:T(2,128)(2,1)}), bf16[16,1,2,2048]{3,2,1,0:T(2,128)(2,1)S(1)}, u32[]{:S(2)}, u32[]{:S(2)}) async-start(bf16[16,1,2,2048]{3,2,1,0:T(2,128)(2,1)} %copy.84), calls=%async_computation.1 | async-start | bytes 262144 | tf_op jit(solution)/shard_map/while/body/eval_jaxpr/all_to_all | solution.py:101
  137.8 6.2 collective-permute-start
  147.7 10.9 %all-to-all-start = ((bf16[16,1,2,2048]{3,2,1,0:T(2,128)(2,1)}), bf16[16,1,2,2048]{3,2,1,0:T(2,128)(2,1)S(1)}, u32[]{:S(2)}, u32[]{:S(2)}) async-start(bf16[16,1,2,2048]{3,2,1,0:T(2,128)(2,1)} %bitcast.324), calls=%async_computation | async-start | bytes 262144 | tf_op jit(solution)/shard_map/while/body/eval_jaxpr/all_to_all | solution.py:118
  162.8 10.9 %all-to-all-start.1 = ((bf16[16,1,2,2048]{3,2,1,0:T(2,128)(2,1)}), bf16[16,1,2,2048]{3,2,1,0:T(2,128)(2,1)S(1)}, u32[]{:S(2)}, u32[]{:S(2)}) async-start(bf16[16,1,2,2048]{3,2,1,0:T(2,128)(2,1)} %copy.84), calls=%async_computation.1 | async-start | bytes 262144 | tf_op jit(solution)/shard_map/while/body/eval_jaxpr/all_to_all | solution.py:101
  174.1 6.2 collective-permute-start
  184.0 10.9 %all-to-all-start = ((bf16[16,1,2,2048]{3,2,1,0:T(2,128)(2,1)}), bf16[16,1,2,2048]{3,2,1,0:T(2,128)(2,1)S(1)}, u32[]{:S(2)}, u32[]{:S(2)}) async-start(bf16[16,1,2,2048]{3,2,1,0:T(2,128)(2,1)} %bitcast.324), calls=%async_computation | async-start | bytes 262144 | tf_op jit(solution)/shard_map/while/body/eval_jaxpr/all_to_all | solution.py:118
  199.1 10.9 %all-to-all-start.1 = ((bf16[16,1,2,2048]{3,2,1,0:T(2,128)(2,1)}), bf16[16,1,2,2048]{3,2,1,0:T(2,128)(2,1)S(1)}, u32[]{:S(2)}, u32[]{:S(2)}) async-start(bf16[16,1,2,2048]{3,2,1,0:T(2,128)(2,1)} %copy.84), calls=%async_computation.1 | async-start | bytes 262144 | tf_op jit(solution)/shard_map/while/body/eval_jaxpr/all_to_all | solution.py:101
  210.4 6.2 collective-permute-start
  220.3 10.9 %all-to-all-start = ((bf16[16,1,2,2048]{3,2,1,0:T(2,128)(2,1)}), bf16[16,1,2,2048]{3,2,1,0:T(2,128)(2,1)S(1)}, u32[]{:S(2)}, u32[]{:S(2)}) async-start(bf16[16,1,2,2048]{3,2,1,0:T(2,128)(2,1)} %bitcast.324), calls=%async_computation | async-start | bytes 262144 | tf_op jit(solution)/shard_map/while/body/eval_jaxpr/all_to_all | solution.py:118
  235.5 10.9 %all-to-all-start.1 = ((bf16[16,1,2,2048]{3,2,1,0:T(2,128)(2,1)}), bf16[16,1,2,2048]{3,2,1,0:T(2,128)(2,1)S(1)}, u32[]{:S(2)}, u32[]{:S(2)}) async-start(bf16[16,1,2,2048]{3,2,1,0:T(2,128)(2,1)} %copy.84), calls=%async_computation.1 | async-start | bytes 262144 | tf_op jit(solution)/shard_map/while/body/eval_jaxpr/all_to_all | solution.py:101
  246.7 6.2 collective-permute-start
  256.7 10.9 %all-to-all-start = ((bf16[16,1,2,2048]{3,2,1,0:T(2,128)(2,1)}), bf16[16,1,2,2048]{3,2,1,0:T(2,128)(2,1)S(1)}, u32[]{:S(2)}, u32[]{:S(2)}) async-start(bf16[16,1,2,2048]{3,2,1,0:T(2,128)(2,1)} %bitcast.324), calls=%async_computation | async-start | bytes 262144 | tf_op jit(solution)/shard_map/while/body/eval_jaxpr/all_to_all | solution.py:118
  271.8 10.9 %all-to-all-start.1 = ((bf16[16,1,2,2048]{3,2,1,0:T(2,128)(2,1)}), bf16[16,1,2,2048]{3,2,1,0:T(2,128)(2,1)S(1)}, u32[]{:S(2)}, u32[]{:S(2)}) async-start(bf16[16,1,2,2048]{3,2,1,0:T(2,128)(2,1)} %copy.84), calls=%async_computation.1 | async-start | bytes 262144 | tf_op jit(solution)/shard_map/while/body/eval_jaxpr/all_to_all | solution.py:101
  283.0 6.2 collective-permute-start
  293.0 10.9 %all-to-all-start = ((bf16[16,1,2,2048]{3,2,1,0:T(2,128)(2,1)}), bf16[16,1,2,2048]{3,2,1,0:T(2,128)(2,1)S(1)}, u32[]{:S(2)}, u32[]{:S(2)}) async-start(bf16[16,1,2,2048]{3,2,1,0:T(2,128)(2,1)} %bitcast.324), calls=%async_computation | async-start | bytes 262144 | tf_op jit(solution)/shard_map/while/body/eval_jaxpr/all_to_all | solution.py:118
  308.1 10.9 %all-to-all-start.1 = ((bf16[16,1,2,2048]{3,2,1,0:T(2,128)(2,1)}), bf16[16,1,2,2048]{3,2,1,0:T(2,128)(2,1)S(1)}, u32[]{:S(2)}, u32[]{:S(2)}) async-start(bf16[16,1,2,2048]{3,2,1,0:T(2,128)(2,1)} %copy.84), calls=%async_computation.1 | async-start | bytes 262144 | tf_op jit(solution)/shard_map/while/body/eval_jaxpr/all_to_all | solution.py:101
  319.4 6.2 collective-permute-start
  329.3 10.9 %all-to-all-start = ((bf16[16,1,2,2048]{3,2,1,0:T(2,128)(2,1)}), bf16[16,1,2,2048]{3,2,1,0:T(2,128)(2,1)S(1)}, u32[]{:S(2)}, u32[]{:S(2)}) async-start(bf16[16,1,2,2048]{3,2,1,0:T(2,128)(2,1)} %bitcast.324), calls=%async_computation | async-start | bytes 262144 | tf_op jit(solution)/shard_map/while/body/eval_jaxpr/all_to_all | solution.py:118
  344.4 10.9 %all-to-all-start.1 = ((bf16[16,1,2,2048]{3,2,1,0:T(2,128)(2,1)}), bf16[16,1,2,2048]{3,2,1,0:T(2,128)(2,1)S(1)}, u32[]{:S(2)}, u32[]{:S(2)}) async-start(bf16[16,1,2,2048]{3,2,1,0:T(2,128)(2,1)} %copy.84), calls=%async_computation.1 | async-start | bytes 262144 | tf_op jit(solution)/shard_map/while/body/eval_jaxpr/all_to_all | solution.py:101
  355.7 6.2 collective-permute-start
  372.2 11.3 %all-to-all-start.2 = ((bf16[16,1,2,2048]{3,2,1,0:T(2,128)(2,1)}), bf16[16,1,2,2048]{3,2,1,0:T(2,128)(2,1)S(1)}, u32[]{:S(2)}, u32[]{:S(2)}) async-start(bf16[16,1,2,2048]{3,2,1,0:T(2,128)(2,1)} %bitcast.359), calls=%async_computation.2 | async-start | bytes 262144 | tf_op jit(solution)/shard_map/while/body/eval_jaxpr/all_to_all | solution.py:162
  388.6 13.3 %all-to-all-start.3 = ((bf16[16,1,2,2048]{3,2,1,0:T(2,128)(2,1)}), bf16[16,1,2,2048]{3,2,1,0:T(2,128)(2,1)S(1)}, u32[]{:S(2)}, u32[]{:S(2)}) async-start(bf16[16,1,2,2048]{3,2,1,0:T(2,128)(2,1)} %copy.87), calls=%async_computation.3 | async-start | bytes 262144 | tf_op jit(solution)/shard_map/while/body/eval_jaxpr/all_to_all | solution.py:167
  404.7 6.1 collective-permute-start.1
  417.1 11.3 %all-to-all-start.2 = ((bf16[16,1,2,2048]{3,2,1,0:T(2,128)(2,1)}), bf16[16,1,2,2048]{3,2,1,0:T(2,128)(2,1)S(1)}, u32[]{:S(2)}, u32[]{:S(2)}) async-start(bf16[16,1,2,2048]{3,2,1,0:T(2,128)(2,1)} %bitcast.359), calls=%async_computation.2 | async-start | bytes 262144 | tf_op jit(solution)/shard_map/while/body/eval_jaxpr/all_to_all | solution.py:162
  428.4 18.6 %copy-start.1 = (f32[2048,16]{0,1:T(8,128)S(1)}, f32[2048,16]{0,1:T(8,128)}, u32[]{:S(2)}) copy-start(f32[2048,16]{0,1:T(8,128)} %get-tuple-element.1229) | copy-start | bytes 393220 | tf_op jit(solution)/shard_map/while
  433.5 13.3 %all-to-all-start.3 = ((bf16[16,1,2,2048]{3,2,1,0:T(2,128)(2,1)}), bf16[16,1,2,2048]{3,2,1,0:T(2,128)(2,1)S(1)}, u32[]{:S(2)}, u32[]{:S(2)}) async-start(bf16[16,1,2,2048]{3,2,1,0:T(2,128)(2,1)} %copy.87), calls=%async_computation.3 | async-start | bytes 262144 | tf_op jit(solution)/shard_map/while/body/eval_jaxpr/all_to_all | solution.py:167
  449.6 6.1 collective-permute-start.1
  462.0 11.3 %all-to-all-start.2 = ((bf16[16,1,2,2048]{3,2,1,0:T(2,128)(2,1)}), bf16[16,1,2,2048]{3,2,1,0:T(2,128)(2,1)S(1)}, u32[]{:S(2)}, u32[]{:S(2)}) async-start(bf16[16,1,2,2048]{3,2,1,0:T(2,128)(2,1)} %bitcast.359), calls=%async_computation.2 | async-start | bytes 262144 | tf_op jit(solution)/shard_map/while/body/eval_jaxpr/all_to_all | solution.py:162
  473.3 18.6 %copy-start.1 = (f32[2048,16]{0,1:T(8,128)S(1)}, f32[2048,16]{0,1:T(8,128)}, u32[]{:S(2)}) copy-start(f32[2048,16]{0,1:T(8,128)} %get-tuple-element.1229) | copy-start | bytes 393220 | tf_op jit(solution)/shard_map/while
  478.4 13.3 %all-to-all-start.3 = ((bf16[16,1,2,2048]{3,2,1,0:T(2,128)(2,1)}), bf16[16,1,2,2048]{3,2,1,0:T(2,128)(2,1)S(1)}, u32[]{:S(2)}, u32[]{:S(2)}) async-start(bf16[16,1,2,2048]{3,2,1,0:T(2,128)(2,1)} %copy.87), calls=%async_computation.3 | async-start | bytes 262144 | tf_op jit(solution)/shard_map/while/body/eval_jaxpr/all_to_all | solution.py:167
  494.5 6.1 collective-permute-start.1
  506.8 11.3 %all-to-all-start.2 = ((bf16[16,1,2,2048]{3,2,1,0:T(2,128)(2,1)}), bf16[16,1,2,2048]{3,2,1,0:T(2,128)(2,1)S(1)}, u32[]{:S(2)}, u32[]{:S(2)}) async-start(bf16[16,1,2,2048]{3,2,1,0:T(2,128)(2,1)} %bitcast.359), calls=%async_computation.2 | async-start | bytes 262144 | tf_op jit(solution)/shard_map/while/body/eval_jaxpr/all_to_all | solution.py:162
  523.2 13.3 %all-to-all-start.3 = ((bf16[16,1,2,2048]{3,2,1,0:T(2,128)(2,1)}), bf16[16,1,2,2048]{3,2,1,0:T(2,128)(2,1)S(1)}, u32[]{:S(2)}, u32[]{:S(2)}) async-start(bf16[16,1,2,2048]{3,2,1,0:T(2,128)(2,1)} %copy.87), calls=%async_computation.3 | async-start | bytes 262144 | tf_op jit(solution)/shard_map/while/body/eval_jaxpr/all_to_all | solution.py:167
  539.3 6.1 collective-permute-start.1
  551.7 11.3 %all-to-all-start.2 = ((bf16[16,1,2,2048]{3,2,1,0:T(2,128)(2,1)}), bf16[16,1,2,2048]{3,2,1,0:T(2,128)(2,1)S(1)}, u32[]{:S(2)}, u32[]{:S(2)}) async-start(bf16[16,1,2,2048]{3,2,1,0:T(2,128)(2,1)} %bitcast.359), calls=%async_computation.2 | async-start | bytes 262144 | tf_op jit(solution)/shard_map/while/body/eval_jaxpr/all_to_all | solution.py:162
  568.1 13.3 %all-to-all-start.3 = ((bf16[16,1,2,2048]{3,2,1,0:T(2,128)(2,1)}), bf16[16,1,2,2048]{3,2,1,0:T(2,128)(2,1)S(1)}, u32[]{:S(2)}, u32[]{:S(2)}) async-start(bf16[16,1,2,2048]{3,2,1,0:T(2,128)(2,1)} %copy.87), calls=%async_computation.3 | async-start | bytes 262144 | tf_op jit(solution)/shard_map/while/body/eval_jaxpr/all_to_all | solution.py:167
  584.2 6.1 collective-permute-start.1
  596.6 11.3 %all-to-all-start.2 = ((bf16[16,1,2,2048]{3,2,1,0:T(2,128)(2,1)}), bf16[16,1,2,2048]{3,2,1,0:T(2,128)(2,1)S(1)}, u32[]{:S(2)}, u32[]{:S(2)}) async-start(bf16[16,1,2,2048]{3,2,1,0:T(2,128)(2,1)} %bitcast.359), calls=%async_computation.2 | async-start | bytes 262144 | tf_op jit(solution)/shard_map/while/body/eval_jaxpr/all_to_all | solution.py:162
  613.0 13.3 %all-to-all-start.3 = ((bf16[16,1,2,2048]{3,2,1,0:T(2,128)(2,1)}), bf16[16,1,2,2048]{3,2,1,0:T(2,128)(2,1)S(1)}, u32[]{:S(2)}, u32[]{:S(2)}) async-start(bf16[16,1,2,2048]{3,2,1,0:T(2,128)(2,1)} %copy.87), calls=%async_computation.3 | async-start | bytes 262144 | tf_op jit(solution)/shard_map/while/body/eval_jaxpr/all_to_all | solution.py:167
  629.1 6.1 collective-permute-start.1
  641.4 11.3 %all-to-all-start.2 = ((bf16[16,1,2,2048]{3,2,1,0:T(2,128)(2,1)}), bf16[16,1,2,2048]{3,2,1,0:T(2,128)(2,1)S(1)}, u32[]{:S(2)}, u32[]{:S(2)}) async-start(bf16[16,1,2,2048]{3,2,1,0:T(2,128)(2,1)} %bitcast.359), calls=%async_computation.2 | async-start | bytes 262144 | tf_op jit(solution)/shard_map/while/body/eval_jaxpr/all_to_all | solution.py:162
  657.9 13.3 %all-to-all-start.3 = ((bf16[16,1,2,2048]{3,2,1,0:T(2,128)(2,1)}), bf16[16,1,2,2048]{3,2,1,0:T(2,128)(2,1)S(1)}, u32[]{:S(2)}, u32[]{:S(2)}) async-start(bf16[16,1,2,2048]{3,2,1,0:T(2,128)(2,1)} %copy.87), calls=%async_computation.3 | async-start | bytes 262144 | tf_op jit(solution)/shard_map/while/body/eval_jaxpr/all_to_all | solution.py:167
  674.0 6.1 collective-permute-start.1
  686.3 11.3 %all-to-all-start.2 = ((bf16[16,1,2,2048]{3,2,1,0:T(2,128)(2,1)}), bf16[16,1,2,2048]{3,2,1,0:T(2,128)(2,1)S(1)}, u32[]{:S(2)}, u32[]{:S(2)}) async-start(bf16[16,1,2,2048]{3,2,1,0:T(2,128)(2,1)} %bitcast.359), calls=%async_computation.2 | async-start | bytes 262144 | tf_op jit(solution)/shard_map/while/body/eval_jaxpr/all_to_all | solution.py:162
  697.7 18.6 %copy-start.1 = (f32[2048,16]{0,1:T(8,128)S(1)}, f32[2048,16]{0,1:T(8,128)}, u32[]{:S(2)}) copy-start(f32[2048,16]{0,1:T(8,128)} %get-tuple-element.1229) | copy-start | bytes 393220 | tf_op jit(solution)/shard_map/while
  702.7 13.3 %all-to-all-start.3 = ((bf16[16,1,2,2048]{3,2,1,0:T(2,128)(2,1)}), bf16[16,1,2,2048]{3,2,1,0:T(2,128)(2,1)S(1)}, u32[]{:S(2)}, u32[]{:S(2)}) async-start(bf16[16,1,2,2048]{3,2,1,0:T(2,128)(2,1)} %copy.87), calls=%async_computation.3 | async-start | bytes 262144 | tf_op jit(solution)/shard_map/while/body/eval_jaxpr/all_to_all | solution.py:167
  718.9 6.1 collective-permute-start.1
  731.2 11.3 %all-to-all-start.2 = ((bf16[16,1,2,2048]{3,2,1,0:T(2,128)(2,1)}), bf16[16,1,2,2048]{3,2,1,0:T(2,128)(2,1)S(1)}, u32[]{:S(2)}, u32[]{:S(2)}) async-start(bf16[16,1,2,2048]{3,2,1,0:T(2,128)(2,1)} %bitcast.359), calls=%async_computation.2 | async-start | bytes 262144 | tf_op jit(solution)/shard_map/while/body/eval_jaxpr/all_to_all | solution.py:162
  742.5 18.6 %copy-start.1 = (f32[2048,16]{0,1:T(8,128)S(1)}, f32[2048,16]{0,1:T(8,128)}, u32[]{:S(2)}) copy-start(f32[2048,16]{0,1:T(8,128)} %get-tuple-element.1229) | copy-start | bytes 393220 | tf_op jit(solution)/shard_map/while
  747.6 13.3 %all-to-all-start.3 = ((bf16[16,1,2,2048]{3,2,1,0:T(2,128)(2,1)}), bf16[16,1,2,2048]{3,2,1,0:T(2,128)(2,1)S(1)}, u32[]{:S(2)}, u32[]{:S(2)}) async-start(bf16[16,1,2,2048]{3,2,1,0:T(2,128)(2,1)} %copy.87), calls=%async_computation.3 | async-start | bytes 262144 | tf_op jit(solution)/shard_map/while/body/eval_jaxpr/all_to_all | solution.py:167
  763.7 6.1 collective-permute-start.1
  770.5 85.5 %reduce-scatter.2.cloned.1.call-start = ((), (), s32[]{:S(2)}) async-start(), calls=%async_computation.5 | async-start | bytes 786432 | tf_op jit(solution)/shard_map/reduce_scatter | solution.py:227
  772.6 37.8 %copy-start.3 = (bf16[8,16,1,2,2048]{4,3,1,2,0:T(2,128)(2,1)S(1)}, bf16[8,16,1,2,2048]{4,3,1,2,0:T(2,128)(2,1)}, u32[]{:S(2)}) copy-start(bf16[8,16,1,2,2048]{4,3,1,2,0:T(2,128)(2,1)} %get-tuple-element.697) | copy-start | bytes 3145732
  772.6 37.8 %copy-start.5 = (bf16[8,16,1,2,512]{4,1,3,2,0:T(8,128)(2,1)S(1)}, bf16[8,16,1,2,512]{4,1,3,2,0:T(8,128)(2,1)}, u32[]{:S(2)}) copy-start(bf16[8,16,1,2,512]{4,1,3,2,0:T(8,128)(2,1)} %get-tuple-element.696) | copy-start | bytes 786436
  (24 other events, 322.1 us)
Sparse Core Ops, SparseCore 0:
  770.7 83.8 all-reduce.1
Sparse Core Ops, SparseCore 1:
  773.8 12.1 reduce-scatter.1
where the time goes:
time: 874 us; the launch traced here: 864 us
  waiting for transfers between devices  227 us (26%)
  starting transfers between devices  200 us (23%)
  matrix products  157 us (18%)
  other arithmetic  120 us (14%)
  local copies, waits for them, and re-layouts  90.7 us (10%)
  blocking collectives  51.4 us (6%)
  between operations  15.6 us (2%)
    dynamic_update_slice x63, other arithmetic, keep_row(): lax.dynamic_update_index_in_dim(stash, jnp.where(active, value, old_row),...  68 us
    all_to_all x9, waiting for transfers between devices, expert_forward(): lax.all_to_all(out_rows, ('expert', 'dp'), split_axis=0, concat_axis=0, t...  59 us
    dot_general x18, matrix products, expert_inner(): jnp.einsum('sekd,edf->sekf', exp_rows, w_gu, preferred_element_type=jnp.f...  54.1 us
    all_to_all x9, starting transfers between devices, backward_tick(): lax.all_to_all(rows_grad, ('expert', 'dp'), split_axis=0, concat_axis=0,...  53.5 us
    ppermute x18, starting transfers between devices, shifted(): lax.ppermute(value, axis, [(source, source + steps) for source in range(l...  49.1 us
    all_to_all x9, waiting for transfers between devices, forward_tick(): lax.all_to_all(send_rows, ('expert', 'dp'), split_axis=0, concat_axis=0,...  46 us
    all_to_all x9, waiting for transfers between devices, backward_tick(): lax.all_to_all(rows_grad, ('expert', 'dp'), split_axis=0, concat_axis=0,...  45.9 us
    psum x1, waiting for transfers between devices, local(): lax.psum(acc_router.astype(jnp.bfloat16), ('expert', 'dp'))  41.1 us
  transfers between devices with their start and end apart: 56, of which 46 were waited for; matrix products, arithmetic and copies ran while one was open for 18% of the time, Pallas kernels for 0%

commit v1 on v0

v1 whole, which is shorter than its diff:
```python
import functools

import jax
import jax.numpy as jnp
from jax import lax
from jax.experimental import pallas as pl
from jax.experimental.pallas import tpu as pltpu
from jax.sharding import PartitionSpec as P

EPS = 1e-05
CHUNKS = 2
LANES = 128
F32 = jnp.float32
BF16 = jnp.bfloat16


def exchange_body(n_arr, n_expert_axis, n_dp_axis, *refs):
    ins, outs = refs[:n_arr], refs[n_arr : 2 * n_arr]
    send_sem, recv_sem = refs[2 * n_arr :]
    n_rank = n_expert_axis * n_dp_axis
    me = lax.axis_index("expert") * n_dp_axis + lax.axis_index("dp")

    def place(step):
        rank = lax.rem(me + step, n_rank)
        return rank, {"expert": lax.div(rank, n_dp_axis), "dp": lax.rem(rank, n_dp_axis)}

    barrier = pltpu.get_barrier_semaphore()
    for step in range(1, n_rank):
        pl.semaphore_signal(
            barrier, inc=1, device_id=place(step)[1], device_id_type=pl.DeviceIdType.MESH
        )
    pl.semaphore_wait(barrier, n_rank - 1)
    copies = []
    for step in range(1, n_rank):
        rank, device = place(step)
        for i in range(n_arr):
            copy = pltpu.make_async_remote_copy(
                src_ref=ins[i].at[rank],
                dst_ref=outs[i].at[me],
                send_sem=send_sem.at[i, step],
                recv_sem=recv_sem.at[i, step],
                device_id=device,
                device_id_type=pl.DeviceIdType.MESH,
            )
            copy.start()
            copies.append(copy)
    for i in range(n_arr):
        outs[i][me] = ins[i][me]
    for copy in copies:
        copy.wait()


def exchange(arrays, collective_id):
    n_rank = arrays[0].shape[0]
    n_expert_axis, n_dp_axis = lax.axis_size("expert"), lax.axis_size("dp")
    spec = pl.BlockSpec(memory_space=pltpu.VMEM)
    return pl.pallas_call(
        functools.partial(exchange_body, len(arrays), n_expert_axis, n_dp_axis),
        out_shape=[jax.ShapeDtypeStruct(a.shape, a.dtype) for a in arrays],
        in_specs=[spec] * len(arrays),
        out_specs=[spec] * len(arrays),
        scratch_shapes=[
            pltpu.SemaphoreType.DMA((len(arrays), n_rank)),
            pltpu.SemaphoreType.DMA((len(arrays), n_rank)),
        ],
        compiler_params=pltpu.CompilerParams(
            collective_id=collective_id, has_side_effects=True
        ),
    )(*arrays)


def dot(a, b, dims, precision=None):
    return lax.dot_general(
        a, b, ((dims[:1], dims[1:]), ((), ())), precision=precision, preferred_element_type=F32
    )


def place_tables(route_all, n_expert, capacity, chunks):
    micro, tok, _ = route_all.shape
    per = micro // chunks
    hits = (route_all[..., None] == jnp.arange(n_expert, dtype=jnp.int32)).astype(jnp.int32)
    named = jnp.sum(hits, axis=2)
    earlier = (jnp.arange(tok)[:, None] > jnp.arange(tok)[None, :]).astype(jnp.int32)
    before = jnp.sum(earlier[None, :, :, None] * named[:, None, :, :], axis=2)
    slot = jnp.sum(hits * before[:, :, None, :], axis=3)
    within = (jnp.arange(micro, dtype=jnp.int32) % per)[:, None, None]
    cell = route_all * (per * capacity) + within * capacity + slot
    cell = jnp.transpose(cell.reshape(chunks, per * tok, 2), (0, 2, 1))
    cells = jnp.arange(n_expert * per * capacity, dtype=jnp.int32)
    tables = (cell[:, :, None, :] == cells[None, None, :, None]).astype(BF16)
    return tables, hits.reshape(chunks, per * tok, 2, n_expert).astype(F32)


def pick(stack, index):
    return lax.dynamic_index_in_dim(stack, index, 0, keepdims=False)


def keep(stack, index, value, active):
    return lax.dynamic_update_index_in_dim(
        stack, jnp.where(active, value, pick(stack, index)), index, 0
    )


def ends_gather(x_in, cotangent, section, n_section):
    if n_section == 1:
        return x_in, cotangent
    x_parts, top_parts = [], []
    last = n_section - 1
    for source in range(n_section):
        if source == 0:
            x_parts.append(x_in)
            continue
        other = last - source
        if other != source:
            got = lax.ppermute(
                jnp.where(section == source, x_in, cotangent),
                "section",
                [(source, 0), (other, last)],
            )
            x_parts.append(got)
            top_parts.append(got)
        else:
            x_parts.append(lax.ppermute(x_in, "section", [(source, 0)]))
            top_parts.append(lax.ppermute(cotangent, "section", [(other, last)]))
    top_parts = top_parts[::-1] + [cotangent]
    return jnp.concatenate(x_parts, axis=2), jnp.concatenate(top_parts, axis=2)


def local(x_in, cotangent, route_ids, norm_gain, router, w_gate_up, w_down):
    micro, tok, _ = x_in.shape
    n_section = lax.axis_size("section")
    n_rank = lax.axis_size("expert") * lax.axis_size("dp")
    per_rank, hidden_width, width = w_down.shape[1:]
    assert per_rank == 1
    n_expert = n_rank
    capacity = tok * 2 * 9 // (8 * n_expert)
    section = lax.axis_index("section")
    last = n_section - 1
    chunks = CHUNKS if n_section > 1 and micro % CHUNKS == 0 else 1
    per = micro // chunks
    tokens = per * tok
    block = per * capacity
    cells = n_rank * block
    gain = norm_gain[0]
    router_mat = router[0]
    router_wide = router_mat.astype(F32)
    w_gu, w_dn = w_gate_up[0, 0], w_down[0, 0]

    x_all, top_all = ends_gather(x_in, cotangent, section, n_section)
    x_all = x_all.reshape(chunks, tokens, width)
    top_all = top_all.reshape(chunks, tokens, width)
    tables, hits_all = place_tables(route_ids[0], n_expert, capacity, chunks)

    zero_rows = jnp.zeros((chunks, cells, width), BF16)
    stash_h = jnp.zeros((chunks, tokens, width), BF16)
    stash_rows, stash_top, stash_dy = zero_rows, zero_rows, zero_rows
    stash_gate = jnp.zeros((chunks, cells), F32)
    stash_hidden = jnp.zeros((chunks, cells, hidden_width), BF16)
    stash_q = jnp.zeros((chunks, cells, 2 * hidden_width), BF16)
    stash_out = jnp.zeros((chunks, tokens, width), BF16)
    acc_router = jnp.zeros((n_expert, width), F32)
    acc_gain = jnp.zeros((width,), F32)
    got_h = jnp.zeros((tokens, width), BF16)
    got_g = jnp.zeros((tokens, width), BF16)

    def both(index):
        return pick(tables, index)[0] + pick(tables, index)[1]

    def blocks(rows):
        return rows.reshape(n_rank, block, rows.shape[-1])

    def lanes(column):
        return jnp.broadcast_to(column[:, None], (cells, LANES)).reshape(n_rank, block, LANES)

    if n_section == 1:
        rows = [blocks(dot(both(c), top_all[c], (1, 0)).astype(BF16)) for c in range(chunks)]
        for c in range(chunks):
            got, _ = exchange([rows[c], lanes(jnp.zeros((cells,), F32))], 0)
            stash_top = stash_top.at[c].set(got.reshape(cells, width))

    for tick in range(chunks + 2 * last):
        any_f = any(0 <= tick - s < chunks for s in range(last))
        any_t = 0 <= tick - last < chunks
        any_b = any(0 <= tick - 2 * last + s < chunks for s in range(last))
        up, down = tick - section, tick - 2 * last + section
        is_top = section == last
        is_f = (up >= 0) & (up < chunks) & ~is_top
        is_t = (up >= 0) & (up < chunks) & is_top
        is_b = (down >= 0) & (down < chunks) & ~is_top
        seed = tick == 0 and n_section > 1
        index = jnp.clip(jnp.where(is_b, down, up), 0, chunks - 1)

        h = got_h
        if tick < chunks:
            h = jnp.where(section == 0, pick(x_all, index), h)
        if any_b:
            h = jnp.where(is_b, pick(stash_h, index), h)
        h_wide = h.astype(F32)
        inv = lax.rsqrt(jnp.mean(h_wide * h_wide, axis=-1, keepdims=True) + EPS)
        u = (h_wide * inv * gain).astype(BF16)
        hits = pick(hits_all, index)
        logits = dot(u, router_mat, (1, 0))
        chosen = jnp.sum(hits * logits[:, None, :], axis=2)
        gate_1 = jax.nn.sigmoid(chosen[:, 0] - chosen[:, 1])
        gate_2 = jax.nn.sigmoid(chosen[:, 1] - chosen[:, 0])
        pair = pick(tables, index)
        first, second = pair[0], pair[1]
        gate_cells = jnp.sum(
            first.astype(F32) * gate_1[None, :] + second.astype(F32) * gate_2[None, :], axis=1
        )
        if any_f or any_t:
            stash_h = keep(stash_h, index, h, is_f | is_t)
        g_top = got_g
        if any_t:
            g_top = jnp.where(is_t, pick(top_all, index), g_top)
        source = u
        if any_b:
            source = jnp.where(is_b, g_top, source) if any_t or any_f else g_top
        if seed:
            source = jnp.where(is_top, top_all[0], source)
        sent = dot(first + second, source, (1, 0)).astype(BF16)
        landed, side = exchange([blocks(sent), lanes(gate_cells)], 0)
        landed = landed.reshape(cells, width)
        gate_here = side.reshape(cells, LANES)[:, 0]
        if seed:
            stash_top = stash_top.at[0].set(jnp.where(is_top, landed, stash_top[0]))
        if any_f or any_t:
            stash_rows = keep(stash_rows, index, landed, is_f | is_t)
            stash_gate = keep(stash_gate, index, gate_here, is_f | is_t)
        if any_b:
            stash_top = keep(stash_top, index, landed, is_b)
        rows, gate_here = pick(stash_rows, index), pick(stash_gate, index)

        gate_up = dot(rows, w_gu, (1, 0))
        a, b = gate_up[:, :hidden_width], gate_up[:, hidden_width:]
        sig = jax.nn.sigmoid(a)
        hidden = (a * sig * b).astype(BF16)
        side_back = jnp.zeros((cells,), F32)
        if any_f:
            y = dot(hidden, w_dn, (1, 0)).astype(BF16)
            reply = y
        if any_t or any_b:
            top_rows = pick(stash_top, index)
            plain = dot(top_rows, w_dn, (1, 1))
            side_back = jnp.sum(plain * hidden.astype(F32), axis=1)
            d_hidden = plain * gate_here[:, None]
            slope = sig * (1.0 + a * (1.0 - sig))
            q = jnp.concatenate([d_hidden * b * slope, d_hidden * (a * sig)], axis=1).astype(BF16)
            dy = (top_rows.astype(F32) * gate_here[:, None]).astype(BF16)
            du_rows = dot(q, w_gu, (1, 1)).astype(BF16)
            stash_q = keep(stash_q, index, q, is_t | is_b)
            stash_dy = keep(stash_dy, index, dy, is_t | is_b)
            stash_hidden = keep(stash_hidden, index, hidden, is_t | is_b)
            reply = jnp.where(is_f, y, du_rows) if any_f else du_rows
        if seed and chunks > 1:
            later = dot(tables[1, 0] + tables[1, 1], top_all[1], (1, 0)).astype(BF16)
            reply = jnp.where(is_top, later, reply)
        back, side = exchange([blocks(reply), lanes(side_back)], 0)
        back = back.reshape(cells, width)
        if seed and chunks > 1:
            stash_top = stash_top.at[1].set(jnp.where(is_top, back, stash_top[1]))
        picked_1 = dot(first, back, (0, 0))
        picked_2 = dot(second, back, (0, 0))
        if any_f:
            h_next = (h_wide + gate_1[:, None] * picked_1 + gate_2[:, None] * picked_2).astype(BF16)
            got_h = lax.ppermute(h_next, "section", [(s, s + 1) for s in range(last)])
        if any_t or any_b:
            c_cells = side.reshape(cells, LANES)[:, :1]
            c_1 = jnp.sum(first.astype(F32) * c_cells, axis=0)
            c_2 = jnp.sum(second.astype(F32) * c_cells, axis=0)
            slope_l = gate_1 * gate_2 * (c_1 - c_2)
            cols = slope_l[:, None] * (hits[:, 0, :] - hits[:, 1, :])
            du = picked_1 + picked_2 + dot(cols, router_wide, (1, 1), lax.Precision.HIGHEST)
            mine = is_t | is_b
            term = dot(cols, u.astype(F32), (0, 0), lax.Precision.HIGHEST)
            acc_router = acc_router + jnp.where(mine, term, 0.0)
            acc_gain = acc_gain + jnp.where(mine, jnp.sum(du * h_wide * inv, axis=0), 0.0)
            scaled = du * gain
            projection = jnp.mean(scaled * h_wide, axis=-1, keepdims=True)
            g_out = (
                g_top.astype(F32) + inv * scaled - h_wide * (inv * inv * inv) * projection
            ).astype(BF16)
            stash_out = keep(stash_out, index, g_out, mine)
            if last > 0 and tick < chunks + 2 * last - 1:
                got_g = lax.ppermute(g_out, "section", [(s, s - 1) for s in range(1, n_section)])

    all_rows = stash_rows.reshape(chunks * cells, width)
    grad_gu = dot(all_rows, stash_q.reshape(chunks * cells, 2 * hidden_width), (0, 0))
    grad_dn = dot(
        stash_hidden.reshape(chunks * cells, hidden_width),
        stash_dy.reshape(chunks * cells, width),
        (0, 0),
    )

    high = -(-(n_expert + 1) // 8) * 8
    piece = width // n_rank
    acc = jnp.concatenate(
        [acc_router, acc_gain[None], jnp.zeros((high - n_expert - 1, width), F32)], axis=0
    )
    parts = jnp.transpose(acc.reshape(high, n_rank, piece), (1, 0, 2))
    (parts,) = exchange([parts], 1)
    total = jnp.broadcast_to(jnp.sum(parts, axis=0)[None], parts.shape)
    (total,) = exchange([total], 1)
    total = jnp.transpose(total, (1, 0, 2)).reshape(high, width)
    grad_router, grad_gain = total[:n_expert].T, total[n_expert]

    out = stash_out.reshape(micro, tok, n_section, width // n_section)
    grad_in = out[:, :, 0]
    for s in range(1, n_section):
        moved = lax.ppermute(out[:, :, s], "section", [(0, s)])
        grad_in = jnp.where(section == s, moved, grad_in)
    return (grad_in, grad_gu[None, None], grad_dn[None, None], grad_router[None], grad_gain[None])


def solution(mesh):
    in_specs = (
        P(None, ("expert", "dp"), "section"),
        P(None, ("expert", "dp"), "section"),
        P("section", None, ("expert", "dp"), None),
        P("section", None),
        P("section", None, None),
        P("section", ("expert", "dp"), None, None),
        P("section", ("expert", "dp"), None, None),
    )
    out_specs = (
        P(None, ("expert", "dp"), "section"),
        P("section", ("expert", "dp"), None, None),
        P("section", ("expert", "dp"), None, None),
        P("section", None, None),
        P("section", None),
    )
    return jax.shard_map(local, mesh=mesh, in_specs=in_specs, out_specs=out_specs, check_vma=False)
```

time: 874 us -> 396 us (0.45)
  waiting for transfers between devices: 227 us -> 10.9 us
  starting transfers between devices: 200 us -> 16.8 us
  Pallas kernels: 0 us -> 179 us
  matrix products: 157 us -> 73.1 us
  other arithmetic: 120 us -> 54.5 us
  blocking collectives: 51.4 us -> 0 us
  local copies, waits for them, and re-layouts: 90.7 us -> 56.9 us
  between operations: 15.6 us -> 1.64 us
    pallas_call x0 -> x10, Pallas kernels: none -> 179 us  [exchange(): pl.pallas_call(functools.partial(exchange_body, len(arrays), n_expert_axi...]
    all_to_all x36 -> x0, starting transfers between devices: 151 us -> none  [the longest x9 53.5 us: backward_tick(): lax.all_to_all(rows_grad, ('expert', 'dp'), split_axis=0, concat_axis=0,...]
    all_to_all x36 -> x0, waiting for transfers between devices: 151 us -> none  [the longest x9 59 us: expert_forward(): lax.all_to_all(out_rows, ('expert', 'dp'), split_axis=0, concat_axis=0, t...]
    dot_general x128 -> x37, matrix products: 157 us -> 73.1 us  [dot(): lax.dot_general(a, b, ((dims[:1], dims[1:]), ((), ())), precision=precisi...]
    dynamic_update_slice x63 -> x14, other arithmetic: 68 us -> 24.2 us  [keep(): lax.dynamic_update_index_in_dim(stack, jnp.where(active, value, pick(stac...]
    psum x1 -> x0, waiting for transfers between devices: 41.1 us -> none  [local(): lax.psum(acc_router.astype(jnp.bfloat16), ('expert', 'dp'))]
    dynamic_slice x54 -> x8, local copies, waits for them, and re-layouts: 41.7 us -> 9.15 us  [pick(): return lax.dynamic_index_in_dim(stack, index, 0, keepdims=False)]
    ppermute x18 -> x6, starting transfers between devices: 49.1 us -> 16.8 us  [the longest x2 9.56 us: local(): got_h = lax.ppermute(h_next, 'section', [(s, s + 1) for s in range(last)])]
  transfers between devices with their start and end apart: 56 -> 6, of which waited for: 46 -> 4; matrix products, arithmetic and copies ran while one was open for 18% -> 9% of each run, Pallas kernels for 0% -> 0%
where the time goes in v1:
time: 396 us; the launch traced here: 393 us
  Pallas kernels  179 us (45%)
  matrix products  73.1 us (18%)
  local copies, waits for them, and re-layouts  56.9 us (14%)
  other arithmetic  54.5 us (14%)
  starting transfers between devices  16.8 us (4%)
  waiting for transfers between devices  10.9 us (3%)
    pallas_call x10, Pallas kernels, exchange(): pl.pallas_call(functools.partial(exchange_body, len(arrays), n_expert_axi...  179 us
    dot_general x37, matrix products, dot(): lax.dot_general(a, b, ((dims[:1], dims[1:]), ((), ())), precision=precisi...  73.1 us
    dynamic_update_slice x14, other arithmetic, keep(): lax.dynamic_update_index_in_dim(stack, jnp.where(active, value, pick(stac...  24.2 us
    broadcast_in_dim x14, local copies, waits for them, and re-layouts, lanes(): jnp.broadcast_to(column[:, None], (cells, LANES))  12.4 us
    unnamed x127, local copies, waits for them, and re-layouts  11.4 us
    ppermute x2, starting transfers between devices, local(): got_h = lax.ppermute(h_next, 'section', [(s, s + 1) for s in range(last)])  9.56 us
    dynamic_slice x8, local copies, waits for them, and re-layouts, pick(): return lax.dynamic_index_in_dim(stack, index, 0, keepdims=False)  9.15 us
    ppermute x2, waiting for transfers between devices, local(): lax.ppermute(g_out, 'section', [(s, s - 1) for s in range(1, n_section)])  8.86 us
  transfers between devices with their start and end apart: 6, of which 4 were waited for; matrix products, arithmetic and copies ran while one was open for 9% of the time, Pallas kernels for 0%

profile of v1, /device:TPU:0, one launch (start us, length us, event | category | flops | bytes accessed | tf_op | source)
XLA Modules:
  0.0 392.7 jit_solution(11858038674358866707)
XLA Ops:
  1.8 3.0 collective-permute-start
  9.5 1.7 collective-permute-done
  17.6 20.7 %shard_map.110 = (bf16[16,8,2048]{2,1,0:T(8,128)(2,1)}, f32[16,8,128]{2,1,0:T(8,128)}) custom-call(bf16[16,8,2048]{2,1,0:T(8,128)(2,1)} %fusion.29.refs_0_, f32[16,8,128]{2,1,0:T(8,128)} %broadcast_in_dim.186.refs_1_), custom_call_target="tpu_custom_call" | custom-call | tf_op jit(solution)/shard_map/pallas_call | solution.py:57
  38.3 1.4 copy.135
  41.0 2.9 fusion.12
  46.2 19.3 %shard_map.111 = (bf16[16,8,2048]{2,1,0:T(8,128)(2,1)}, f32[16,8,128]{2,1,0:T(8,128)}) custom-call(bf16[16,8,2048]{2,1,0:T(8,128)(2,1)} %fusion.40.refs_0_, f32[16,8,128]{2,1,0:T(8,128)} %reshape.844.refs_1_), custom_call_target="tpu_custom_call" | custom-call | tf_op jit(solution)/shard_map/pallas_call | solution.py:57
  69.2 4.3 %collective-permute-start.1 = (bf16[64,2048]{1,0:T(8,128)(2,1)S(1)}, bf16[64,2048]{1,0:T(8,128)(2,1)}, u32[]{:S(2)}, u32[]{:S(2)}) collective-permute-start(bf16[64,2048]{1,0:T(8,128)(2,1)S(1)} %fusion.41), channel_id=1, source_target_pairs={{0,16},{1,17},{2,18},{3,19},{4,20},{5,21},{6,22},{7,23},{8,24},{9,... | collective-permute-start | bytes 786440 | tf_op jit(solution)/shard_map/ppermute | solution.py:266
  73.5 1.7 constant_dynamic-slice_fusion.16
  75.9 2.3 pad_maximum_fusion
  78.5 1.8 bitcast_dynamic-update-slice_fusion.3
  86.5 19.7 %shard_map.112 = (bf16[16,8,2048]{2,1,0:T(8,128)(2,1)}, f32[16,8,128]{2,1,0:T(8,128)}) custom-call(bf16[16,8,2048]{2,1,0:T(8,128)(2,1)} %fusion.30.refs_0_, f32[16,8,128]{2,1,0:T(8,128)} %broadcast_in_dim.188.refs_1_), custom_call_target="tpu_custom_call" | custom-call | tf_op jit(solution)/shard_map/pallas_call | solution.py:57
  110.9 2.9 fusion.10
  115.4 1.6 copy.125
  117.1 3.3 multiply_convert_fusion.12
  121.1 3.9 fusion.14
  127.0 19.6 %shard_map.113 = (bf16[16,8,2048]{2,1,0:T(8,128)(2,1)}, f32[16,8,128]{2,1,0:T(8,128)}) custom-call(bf16[16,8,2048]{2,1,0:T(8,128)(2,1)} %fusion.39.refs_0_, f32[16,8,128]{2,1,0:T(8,128)} %broadcast_in_dim.191.refs_1_), custom_call_target="tpu_custom_call" | custom-call | tf_op jit(solution)/shard_map/pallas_call | solution.py:57
  148.0 2.4 fusion.85
  150.3 5.3 %collective-permute-start.3 = (bf16[64,2048]{1,0:T(8,128)(2,1)}, bf16[64,2048]{1,0:T(8,128)(2,1)}, u32[]{:S(2)}, u32[]{:S(2)}) collective-permute-start(bf16[64,2048]{1,0:T(8,128)(2,1)} %get-tuple-element.135), channel_id=1, source_target_pairs={{0,16},{1,17},{2,18},{3,19},{4,20},{5,21},{6,22},{7,23},{8,24},{9,... | collective-permute-start | bytes 786440 | tf_op jit(solution)/shard_map/ppermute | solution.py:266
  159.0 1.4 copy.137
  171.0 1.7 bitcast_dynamic-update-slice_fusion.4
  177.3 1.9 convolution_select_fusion.2
  179.2 3.1 collective-permute-done.2
  182.3 2.2 fusion.31.refs_0_
  185.9 19.9 %shard_map.114 = (bf16[16,8,2048]{2,1,0:T(8,128)(2,1)}, f32[16,8,128]{2,1,0:T(8,128)}) custom-call(bf16[16,8,2048]{2,1,0:T(8,128)(2,1)} %fusion.31.refs_0_, f32[16,8,128]{2,1,0:T(8,128)} %broadcast_in_dim.195.refs_1_), custom_call_target="tpu_custom_call" | custom-call | tf_op jit(solution)/shard_map/pallas_call | solution.py:57
  206.0 3.1 fusion.72
  209.1 1.5 fusion.2
  210.7 1.6 fusion.6
  212.2 1.4 copy.138
  217.4 1.9 fusion.150
  219.3 1.7 copy.127
  221.0 1.5 constant_dynamic-update-slice_fusion.1
  222.5 3.3 multiply_convert_fusion.10
  227.1 1.6 constant_dynamic-slice_fusion.1
  228.7 1.7 copy.128
  230.3 1.9 fusion.149
  232.2 1.7 copy.129
  233.9 4.7 %fusion.36.refs_0_ = bf16[16,8,2048]{2,1,0:T(8,128)(2,1)} fusion(bf16[1,1,2048,1024]{3,2,1,0:T(8,128)(2,1)} %param.16, bf16[128,512]{1,0:T(8,128)(2,1)} %get-tuple-element.102, bf16[128,512]{1,0:T(8,128)(2,1)} %get-tuple-element.101), kind=kOutput, calls=%fused_computation.41 | convolution fusion | flops 537657344 | bytes 4980736 | tf_op jit(solution)/shard_map/dot_general | solution.py:73
  239.3 19.3 %shard_map.115 = (bf16[16,8,2048]{2,1,0:T(8,128)(2,1)}, f32[16,8,128]{2,1,0:T(8,128)}) custom-call(bf16[16,8,2048]{2,1,0:T(8,128)(2,1)} %fusion.36.refs_0_, f32[16,8,128]{2,1,0:T(8,128)} %broadcast_in_dim.197.refs_1_), custom_call_target="tpu_custom_call" | custom-call | tf_op jit(solution)/shard_map/pallas_call | solution.py:57
  258.6 1.4 copy.139
  264.1 2.0 fusion.61
  266.1 2.0 bitcast_dynamic-update-slice_fusion.2
  268.1 1.7 constant_dynamic-slice_fusion.4
  269.8 1.5 collective-permute-start.4
  271.3 1.7 fusion.139
  274.1 5.8 %collective-permute-done.4 = bf16[64,2048]{1,0:T(8,128)(2,1)S(1)} collective-permute-done((bf16[64,2048]{1,0:T(8,128)(2,1)S(1)}, bf16[64,2048]{1,0:T(8,128)(2,1)S(1)}, u32[]{:S(2)}, u32[]{:S(2)}) %collective-permute-start.4) | collective-permute-done | bytes 262176 | tf_op jit(solution)/shard_map/ppermute | solution.py:285
  282.4 19.7 %shard_map.116 = (bf16[16,8,2048]{2,1,0:T(8,128)(2,1)}, f32[16,8,128]{2,1,0:T(8,128)}) custom-call(bf16[16,8,2048]{2,1,0:T(8,128)(2,1)} %fusion.32.refs_0_, f32[16,8,128]{2,1,0:T(8,128)} %broadcast_in_dim.201.refs_1_), custom_call_target="tpu_custom_call" | custom-call | tf_op jit(solution)/shard_map/pallas_call | solution.py:57
  302.1 2.9 fusion.74
  305.0 3.3 multiply_convert_fusion.7
  309.7 4.7 %fusion.33.refs_0_ = bf16[16,8,2048]{2,1,0:T(8,128)(2,1)} fusion(bf16[1,1,2048,1024]{3,2,1,0:T(8,128)(2,1)} %param.16, bf16[128,512]{1,0:T(8,128)(2,1)} %get-tuple-element.100, bf16[128,512]{1,0:T(8,128)(2,1)} %get-tuple-element.99), kind=kOutput, calls=%fused_computation.40 | convolution fusion | flops 537657344 | bytes 4980736 | tf_op jit(solution)/shard_map/dot_general | solution.py:73
  315.0 19.6 %shard_map.117 = (bf16[16,8,2048]{2,1,0:T(8,128)(2,1)}, f32[16,8,128]{2,1,0:T(8,128)}) custom-call(bf16[16,8,2048]{2,1,0:T(8,128)(2,1)} %fusion.33.refs_0_, f32[16,8,128]{2,1,0:T(8,128)} %broadcast_in_dim.203.refs_1_), custom_call_target="tpu_custom_call" | custom-call | tf_op jit(solution)/shard_map/pallas_call | solution.py:57
  334.6 1.4 copy.140
  341.2 2.3 fusion.70
  344.2 10.7 %shard_map.118 = f32[16,24,128]{2,1,0:T(8,128)} custom-call(f32[16,24,128]{2,1,0:T(8,128)} %maximum_bitcast_fusion.refs_0_), custom_call_target="tpu_custom_call" | custom-call | tf_op jit(solution)/shard_map/pallas_call | solution.py:57
  356.6 10.4 %shard_map.119 = f32[16,24,128]{2,1,0:T(8,128)} custom-call(f32[16,24,128]{2,1,0:T(8,128)} %broadcast_in_dim.215.refs_0_), custom_call_target="tpu_custom_call" | custom-call | tf_op jit(solution)/shard_map/pallas_call | solution.py:57
  366.9 1.4 slice_bitcast_fusion.1
  368.4 1.6 bitcast_bitcast_fusion
  370.0 2.2 fusion.76
  372.2 2.2 fusion.127
  374.4 2.3 reshape.864
  376.7 2.2 fusion.252
  379.0 1.5 collective-permute-start.5
  380.5 4.0 %convolution_bitcast_fusion.1 = f32[1,1,512,2048]{3,2,1,0:T(8,128)} fusion(bf16[2,128,512]{1,2,0:T(8,128)(2,1)S(1)} %copy-done.17, bf16[2,128,2048]{2,1,0:T(8,128)(2,1)} %fusion.76), kind=kOutput, calls=%fused_computation.15 | convolution fusion | flops 536870912 | bytes 5505024 | tf_op jit(solution)/shard_map/dot_general | solution.py:73
  384.5 1.7 fusion.140
  386.2 5.7 %convolution_bitcast_fusion = f32[1,1,2048,1024]{3,2,1,0:T(8,128)} fusion(bf16[2,128,2048]{2,1,0:T(8,128)(2,1)S(1)} %get-tuple-element.105, bf16[2,128,1024]{2,1,0:T(8,128)(2,1)} %fusion.140), kind=kOutput, calls=%fused_computation | convolution fusion | flops 1073741824 | bytes 9961472 | tf_op jit(solution)/shard_map/dot_general | solution.py:73
  (243 shorter events, 80.4 us)
Async XLA Ops:
  0.6 43.2 %copy-start = (bf16[1,1,512,2048]{3,2,1,0:T(8,128)(2,1)S(1)}, bf16[1,1,512,2048]{3,2,1,0:T(8,128)(2,1)}, u32[]{:S(2)}) copy-start(bf16[1,1,512,2048]{3,2,1,0:T(8,128)(2,1)} %param.17) | copy-start | bytes 6291460
  0.6 13.2 %copy-start.21 = (bf16[8,16,1024]{2,1,0:T(8,128)(2,1)S(1)}, bf16[8,16,1024]{2,1,0:T(8,128)(2,1)}, u32[]{:S(2)}) copy-start(bf16[8,16,1024]{2,1,0:T(8,128)(2,1)} %param.12) | copy-start | bytes 786436
  0.7 14.9 %copy-start.23 = (f32[1,2048]{1,0:T(1,128)S(1)}, f32[1,2048]{1,0:T(1,128)}, u32[]{:S(2)}) copy-start(f32[1,2048]{1,0:T(1,128)} %param.14) | copy-start | bytes 24580
  1.8 9.3 %collective-permute-start = (bf16[8,16,1024]{2,1,0:T(8,128)(2,1)S(1)}, bf16[8,16,1024]{2,1,0:T(8,128)(2,1)S(1)}, u32[]{:S(2)}, u32[]{:S(2)}) collective-permute-start(bf16[8,16,1024]{2,1,0:T(8,128)(2,1)S(1)} %broadcast_select_fusion), channel_id=1, source_target_pairs={{16,0},{0,16},{17,1},{1,17},{18,2},{2,18},{19,3},{3,19},{20,4},{4,... | collective-permute-start | bytes 786440 | tf_op jit(solution)/shard_map/ppermute | solution.py:115
  5.8 9.8 %copy-start.33 = (f32[2,64,2,16]{1,3,2,0:T(8,128)}, f32[2,64,2,16]{1,3,2,0:T(8,128)S(1)}, u32[]{:S(2)}) copy-start(f32[2,64,2,16]{1,3,2,0:T(8,128)S(1)} %convert_convert_fusion) | copy-start | bytes 49156
  12.2 27.5 %copy-start.5 = (bf16[8,16,2048]{2,1,0:T(8,128)(2,1)}, bf16[8,16,2048]{2,1,0:T(8,128)(2,1)S(1)}, u32[]{:S(2)}) copy-start(bf16[8,16,2048]{2,1,0:T(8,128)(2,1)S(1)} %pad_maximum_fusion.1) | copy-start | bytes 1572868
  13.9 1.7 copy-start.7
  65.5 15.6 %copy-start.24 = (bf16[1,2048,16]{1,2,0:T(8,128)(2,1)S(1)}, bf16[1,2048,16]{1,2,0:T(8,128)(2,1)}, u32[]{:S(2)}) copy-start(bf16[1,2048,16]{1,2,0:T(8,128)(2,1)} %param.15) | copy-start | bytes 196612
  69.2 9.3 %collective-permute-start.1 = (bf16[64,2048]{1,0:T(8,128)(2,1)S(1)}, bf16[64,2048]{1,0:T(8,128)(2,1)}, u32[]{:S(2)}, u32[]{:S(2)}) collective-permute-start(bf16[64,2048]{1,0:T(8,128)(2,1)S(1)} %fusion.41), channel_id=1, source_target_pairs={{0,16},{1,17},{2,18},{3,19},{4,20},{5,21},{6,22},{7,23},{8,24},{9,... | collective-permute-start | bytes 786440 | tf_op jit(solution)/shard_map/ppermute | solution.py:266
  75.9 8.0 %copy-start.53 = (f32[2,128]{1,0:T(2,128)}, f32[2,128]{1,0:T(2,128)S(1)}, u32[]{:S(2)}) copy-start(f32[2,128]{1,0:T(2,128)S(1)} %dynamic_update_slice.76) | copy-start | bytes 3076
  80.4 67.6 %copy-start.3 = (bf16[64,2048]{1,0:T(8,128)(2,1)}, bf16[64,2048]{1,0:T(8,128)(2,1)S(1)}, u32[]{:S(2)}) copy-start(bf16[64,2048]{1,0:T(8,128)(2,1)S(1)} %get-tuple-element.92) | copy-start | bytes 786436
  81.1 2.8 copy-start.52
  83.8 0.6 copy-start.40
  83.8 0.6 copy-start.42
  110.9 9.5 %copy-start.58 = (f32[128]{0:T(128)}, f32[128]{0:T(128)S(1)}, u32[]{:S(2)}) copy-start(f32[128]{0:T(128)S(1)} %fusion.228) | copy-start | bytes 1540
  113.8 0.8 copy-start.19
  121.1 3.9 copy-start.32
  146.6 10.9 %copy-start.30 = (bf16[128,512]{1,0:T(8,128)(2,1)S(1)}, bf16[128,512]{1,0:T(8,128)(2,1)}, u32[]{:S(2)}) copy-start(bf16[128,512]{1,0:T(8,128)(2,1)} %get-tuple-element.103) | copy-start | bytes 393220
  146.6 10.9 %copy-start.31 = (bf16[128,512]{1,0:T(8,128)(2,1)S(1)}, bf16[128,512]{1,0:T(8,128)(2,1)}, u32[]{:S(2)}) copy-start(bf16[128,512]{1,0:T(8,128)(2,1)} %get-tuple-element.104) | copy-start | bytes 393220
  147.9 2.4 copy-start.10
  147.9 21.4 %copy-start.41 = (f32[64,1]{0,1:T(1,128)S(1)}, f32[64,1]{0,1:T(1,128)}, u32[]{:S(2)}) copy-start(f32[64,1]{0,1:T(1,128)} %copy-done.40) | copy-start | bytes 772
  148.0 21.4 %copy-start.43 = (f32[64,1]{0,1:T(1,128)S(1)}, f32[64,1]{0,1:T(1,128)}, u32[]{:S(2)}) copy-start(f32[64,1]{0,1:T(1,128)} %copy-done.42) | copy-start | bytes 772
  150.3 11.3 %collective-permute-start.3 = (bf16[64,2048]{1,0:T(8,128)(2,1)}, bf16[64,2048]{1,0:T(8,128)(2,1)}, u32[]{:S(2)}, u32[]{:S(2)}) collective-permute-start(bf16[64,2048]{1,0:T(8,128)(2,1)} %get-tuple-element.135), channel_id=1, source_target_pairs={{0,16},{1,17},{2,18},{3,19},{4,20},{5,21},{6,22},{7,23},{8,24},{9,... | collective-permute-start | bytes 786440 | tf_op jit(solution)/shard_map/ppermute | solution.py:266
  156.6 1.7 copy-start.14
  160.5 8.9 %copy-start.4 = (bf16[64,2048]{1,0:T(8,128)(2,1)S(1)}, bf16[64,2048]{1,0:T(8,128)(2,1)}, u32[]{:S(2)}) copy-start(bf16[64,2048]{1,0:T(8,128)(2,1)} %copy-done.3) | copy-start | bytes 786436
  160.5 8.9 %copy-start.11 = (f32[64,2048]{1,0:T(8,128)S(1)}, f32[64,2048]{1,0:T(8,128)}, u32[]{:S(2)}) copy-start(f32[64,2048]{1,0:T(8,128)} %copy-done.10) | copy-start | bytes 1572868
  160.5 8.9 %copy-start.18 = (f32[64,2048]{1,0:T(8,128)S(1)}, f32[64,2048]{1,0:T(8,128)}, u32[]{:S(2)}) copy-start(f32[64,2048]{1,0:T(8,128)} %get-tuple-element.136) | copy-start | bytes 1572868
  160.5 10.5 %copy-start.8 = (bf16[8,16,2048]{2,1,0:T(8,128)(2,1)S(1)}, bf16[8,16,2048]{2,1,0:T(8,128)(2,1)}, u32[]{:S(2)}) copy-start(bf16[8,16,2048]{2,1,0:T(8,128)(2,1)} %copy-done.7) | copy-start | bytes 1572868
  164.7 6.1 %copy-start.12 = (bf16[64,2048]{1,0:T(8,128)(2,1)}, bf16[64,2048]{1,0:T(8,128)(2,1)S(1)}, u32[]{:S(2)}) copy-start(bf16[64,2048]{1,0:T(8,128)(2,1)S(1)} %get-tuple-element.90) | copy-start | bytes 786436
  165.3 5.5 %copy-start.50 = (f32[64]{0:T(128)}, f32[64]{0:T(128)S(1)}, u32[]{:S(2)}) copy-start(f32[64]{0:T(128)S(1)} %get-tuple-element.130) | copy-start | bytes 772
  168.0 2.8 copy-start.48
  168.0 2.8 copy-start.49
  168.0 2.8 copy-start.46
  168.1 2.8 copy-start.47
  169.4 1.5 copy-start.55
  172.6 1.3 copy-start.6
  172.6 9.7 %collective-permute-start.2 = (bf16[64,2048]{1,0:T(8,128)(2,1)}, bf16[64,2048]{1,0:T(8,128)(2,1)}, u32[]{:S(2)}, u32[]{:S(2)}) collective-permute-start(bf16[64,2048]{1,0:T(8,128)(2,1)} %get-tuple-element.82), channel_id=1, source_target_pairs={{16,0},{17,1},{18,2},{19,3},{20,4},{21,5},{22,6},{23,7},{24,8},{25... | collective-permute-start | bytes 786440 | tf_op jit(solution)/shard_map/ppermute | solution.py:285
  205.9 3.3 copy-start.1
  209.1 3.1 copy-start.2
  233.9 4.7 %copy-start.38 = (f32[16,8]{1,0:T(8,128)S(1)}, f32[16,8]{1,0:T(8,128)}, u32[]{:S(2)}) copy-start(f32[16,8]{1,0:T(8,128)} %broadcast_in_dim.196) | copy-start | bytes 1540
  260.1 6.0 %copy-start.9 = (bf16[8,16,2048]{2,1,0:T(8,128)(2,1)S(1)}, bf16[8,16,2048]{2,1,0:T(8,128)(2,1)}, u32[]{:S(2)}) copy-start(bf16[8,16,2048]{2,1,0:T(8,128)(2,1)} %copy-done.7) | copy-start | bytes 1572868
  260.1 6.1 %copy-start.20 = (bf16[1,64,2048]{2,1,0:T(8,128)(2,1)S(1)}, bf16[1,64,2048]{2,1,0:T(8,128)(2,1)}, u32[]{:S(2)}) copy-start(bf16[1,64,2048]{2,1,0:T(8,128)(2,1)} %constant_dynamic-slice_fusion.9) | copy-start | bytes 786436
  260.1 11.2 %copy-start.27 = (bf16[128,512]{1,0:T(8,128)(2,1)S(1)}, bf16[128,512]{1,0:T(8,128)(2,1)}, u32[]{:S(2)}) copy-start(bf16[128,512]{1,0:T(8,128)(2,1)} %get-tuple-element.101) | copy-start | bytes 393220
  260.1 11.2 %copy-start.28 = (bf16[128,512]{1,0:T(8,128)(2,1)S(1)}, bf16[128,512]{1,0:T(8,128)(2,1)}, u32[]{:S(2)}) copy-start(bf16[128,512]{1,0:T(8,128)(2,1)} %get-tuple-element.102) | copy-start | bytes 393220
  260.1 13.0 %copy-start.15 = (bf16[2,128,512]{1,2,0:T(8,128)(2,1)S(1)}, bf16[2,128,512]{1,2,0:T(8,128)(2,1)}, u32[]{:S(2)}) copy-start(bf16[2,128,512]{1,2,0:T(8,128)(2,1)} %constant_dynamic-update-slice_fusion.1) | copy-start | bytes 786436
  260.1 13.0 %copy-start.29 = (bf16[1,128,512]{1,2,0:T(8,128)(2,1)S(1)}, bf16[1,128,512]{1,2,0:T(8,128)(2,1)}, u32[]{:S(2)}) copy-start(bf16[1,128,512]{1,2,0:T(8,128)(2,1)} %copy.129) | copy-start | bytes 393220
  260.1 13.0 %copy-start.34 = (f32[16,2048]{1,0:T(8,128)S(1)}, f32[16,2048]{1,0:T(8,128)}, u32[]{:S(2)}) copy-start(f32[16,2048]{1,0:T(8,128)} %convolution_select_fusion.2) | copy-start | bytes 393220
  260.1 13.0 %copy-start.35 = (f32[64,2,16]{0,2,1:T(8,128)S(1)}, f32[64,2,16]{0,2,1:T(8,128)}, u32[]{:S(2)}) copy-start(f32[64,2,16]{0,2,1:T(8,128)} %get-tuple-element.84) | copy-start | bytes 24580
  260.1 13.0 %copy-start.45 = (f32[64]{0:T(128)S(1)}, f32[64]{0:T(128)}, u32[]{:S(2)}) copy-start(f32[64]{0:T(128)} %copy-done.44) | copy-start | bytes 772
  262.3 19.4 %copy-start.37 = (f32[16,8]{1,0:T(8,128)S(1)}, f32[16,8]{1,0:T(8,128)}, u32[]{:S(2)}) copy-start(f32[16,8]{1,0:T(8,128)} %broadcast_in_dim.200) | copy-start | bytes 1540
  269.8 10.1 %collective-permute-start.4 = (bf16[64,2048]{1,0:T(8,128)(2,1)S(1)}, bf16[64,2048]{1,0:T(8,128)(2,1)S(1)}, u32[]{:S(2)}, u32[]{:S(2)}) collective-permute-start(bf16[64,2048]{1,0:T(8,128)(2,1)S(1)} %get-tuple-element.80), channel_id=1, source_target_pairs={{16,0},{17,1},{18,2},{19,3},{20,4},{21,5},{22,6},{23,7},{24,8},{25... | collective-permute-start | bytes 786440 | tf_op jit(solution)/shard_map/ppermute | solution.py:285
  273.1 1.0 copy-start.16
  279.9 0.7 copy-start.22
  308.4 30.2 %copy-start.13 = (bf16[64,2048]{1,0:T(8,128)(2,1)S(1)}, bf16[64,2048]{1,0:T(8,128)(2,1)}, u32[]{:S(2)}) copy-start(bf16[64,2048]{1,0:T(8,128)(2,1)} %copy-done.12) | copy-start | bytes 786436
  309.7 4.7 %copy-start.39 = (f32[16,8]{1,0:T(8,128)S(1)}, f32[16,8]{1,0:T(8,128)}, u32[]{:S(2)}) copy-start(f32[16,8]{1,0:T(8,128)} %broadcast_in_dim.202) | copy-start | bytes 1540
  336.0 7.4 %copy-start.36 = (f32[2048]{0:T(1024)S(1)}, f32[2048]{0:T(1024)}, u32[]{:S(2)}) copy-start(f32[2048]{0:T(1024)} %get-tuple-element.59) | copy-start | bytes 24580
  336.0 7.4 %copy-start.56 = (f32[24]{0:T(128)S(1)}, f32[24]{0:T(128)}, u32[]{:S(2)}) copy-start(f32[24]{0:T(128)} %pad.7.clone) | copy-start | bytes 292
  336.7 33.2 %copy-start.54 = (f32[128]{0:T(128)S(1)}, f32[128]{0:T(128)}, u32[]{:S(2)}) copy-start(f32[128]{0:T(128)} %get-tuple-element.119) | copy-start | bytes 1540
  336.8 35.4 %copy-start.51 = (f32[64]{0:T(128)S(1)}, f32[64]{0:T(128)}, u32[]{:S(2)}) copy-start(f32[64]{0:T(128)} %copy-done.50) | copy-start | bytes 772
  336.8 35.4 %copy-start.57 = (f32[64]{0:T(128)S(1)}, f32[64]{0:T(128)}, u32[]{:S(2)}) copy-start(f32[64]{0:T(128)} %get-tuple-element.129) | copy-start | bytes 772
  374.4 6.1 %copy-start.17 = (bf16[2,128,512]{1,2,0:T(8,128)(2,1)S(1)}, bf16[2,128,512]{1,2,0:T(8,128)(2,1)}, u32[]{:S(2)}) copy-start(bf16[2,128,512]{1,2,0:T(8,128)(2,1)} %copy-done.16) | copy-start | bytes 786436
  376.7 7.8 %copy-start.25 = (bf16[128,512]{1,0:T(8,128)(2,1)S(1)}, bf16[128,512]{1,0:T(8,128)(2,1)}, u32[]{:S(2)}) copy-start(bf16[128,512]{1,0:T(8,128)(2,1)} %get-tuple-element.99) | copy-start | bytes 393220
  376.7 7.8 %copy-start.26 = (bf16[128,512]{1,0:T(8,128)(2,1)S(1)}, bf16[128,512]{1,0:T(8,128)(2,1)}, u32[]{:S(2)}) copy-start(bf16[128,512]{1,0:T(8,128)(2,1)} %get-tuple-element.100) | copy-start | bytes 393220
  379.0 12.9 %collective-permute-start.5 = (bf16[8,16,1024]{2,1,0:T(8,128)(2,1)S(1)}, bf16[8,16,1024]{2,1,0:T(8,128)(2,1)S(1)}, u32[]{:S(2)}, u32[]{:S(2)}) collective-permute-start(bf16[8,16,1024]{2,1,0:T(8,128)(2,1)S(1)} %bitcast.478), channel_id=1, source_target_pairs={{0,16},{1,17},{2,18},{3,19},{4,20},{5,21},{6,22},{7,23},{8,24},{9,... | collective-permute-start | bytes 786440 | tf_op jit(solution)/shard_map/ppermute | solution.py:310
  (1 other events, 0.5 us)
